TPU v7x, 32 devices: a whole 2x2x4 slice. The times are simulated.
32 devices in a mesh: gx: 8 (over y, x, core), gy: 4 (over z).
Axes of the slice: x: 2, y: 2, z: 4, core: 2. Of those that a mesh axis runs over, the one named last changes fastest.
Arguments:
- source_field: bfloat16 [4096, 128, 128], P(('gx', 'gy')), may hold values from -6 to 6
- weight_blocks: bfloat16 [16384, 128, 128], P(('gx', 'gy')), may hold values from -0.1875 to 0.1875
- source_ids: int32 [16384], replicated, may hold values from 0 to 4095, as said below
- target_ids: int32 [16384], replicated, may hold values from 0 to 2047, as said below
Outputs:
- remapped: bfloat16 [2048, 128, 128], P(('gx', 'gy'))
Inputs may be any that keep to these rules, and one draw needn't show every extreme that they name: `source_ids`: source block b lies on device b // 128 of gx+gy, and weight block k lies on device k // 512. The weight blocks of device d name only source blocks of devices d - 2 to d + 2. Among the weight blocks of one device, at most 64 distinct source blocks of any one other device are named, and exactly 64 for some other device. `target_ids`: target block t lies on device t // 64 of gx+gy. The weight blocks of device d name only target blocks of devices d - 2 to d + 2. Among the weight blocks of one device, at most 16 distinct target blocks of any one device are named, and exactly 16 for some other device.
All inputs are finite; a program needn't handle non-finite values.
Results may differ from a plain program's by a relative error of at most 0.001.
Values may be sent and summed in bfloat16 or wider, within the bound.
A program may use at most 192 MiB of HBM per device.

v0:
```python
import jax
import jax.numpy as jnp
from jax import lax
from jax.sharding import PartitionSpec as P

HALF = 2
TB_DEV = 64
CAP_S = 64
CAP_T = 16


def passed_along(value, axis, steps):
    count = lax.axis_size(axis)
    initial, last = (max(0, -steps), min(count, count - steps))
    return lax.ppermute(value, axis, [(source, source + steps) for source in range(initial, last)])


def slot_table(wanted, slot_count, per_device):
    ranks = jnp.cumsum(wanted, axis=1) - 1
    matches = (wanted[:, None, :] == 1) & (
        ranks[:, None, :] == jnp.arange(slot_count, dtype=jnp.int32)[None, :, None]
    )
    chosen = jnp.sum(
        matches.astype(jnp.int32) * jnp.arange(per_device, dtype=jnp.int32)[None, None, :], axis=2
    )
    filled = jnp.any(matches, axis=2)
    return (chosen.reshape(-1), filled.reshape(-1))


def rows_of(ids, device, devices, held):
    clamped = jnp.clip(device, 0, devices - 1)
    return lax.dynamic_slice_in_dim(ids, clamped * held, held, 0)


def picked_for(rows, per_device, slot_count, owner_id):
    owner = rows // per_device
    local = rows % per_device
    asked = (
        jnp.zeros((1, per_device), jnp.int32)
        .at[0, local]
        .max((owner == owner_id).astype(jnp.int32))
    )
    return slot_table(asked, slot_count, per_device)


def ranked(relative, local, per_device):
    span = 2 * HALF + 1
    table = jnp.zeros((span, per_device), jnp.int32).at[relative + HALF, local].set(1)
    rank = jnp.cumsum(table, axis=1) - 1
    return rank[relative + HALF, local]


def body(source_field, weight_blocks, source_ids, target_ids):
    devices = lax.axis_size(("gx", "gy"))
    myself = lax.axis_index(("gx", "gy"))
    held = weight_blocks.shape[0]
    src_count = source_field.shape[0]
    span = 2 * HALF + 1
    own_src = rows_of(source_ids, myself, devices, held)
    own_rel = own_src // src_count - myself
    own_local = own_src % src_count
    pieces = []
    bases = []
    offset = 0
    for relative in range(-HALF, HALF + 1):
        bases.append(offset)
        if relative == 0:
            pieces.append(source_field)
            offset = offset + src_count
        else:
            step = -relative
            rows = rows_of(source_ids, myself + step, devices, held)
            chosen, filled = picked_for(rows, src_count, CAP_S, myself)
            outgoing = jnp.where(
                filled[:, None, None], source_field[chosen], jnp.zeros((), jnp.bfloat16)
            )
            pieces.append(passed_along(outgoing, ("gx", "gy"), step))
            offset = offset + CAP_S
    table = jnp.concatenate(pieces, axis=0)
    base_table = jnp.array(bases, dtype=jnp.int32)
    rank = ranked(own_rel, own_local, src_count)
    index = jnp.where(own_rel == 0, base_table[HALF] + own_local, base_table[own_rel + HALF] + rank)
    gathered = table[index]
    partial_value = jnp.einsum(
        "kts,ksc->ktc", weight_blocks, gathered, preferred_element_type=jnp.float32
    )
    own_tgt = rows_of(target_ids, myself, devices, held)
    tgt_rel = own_tgt // TB_DEV - myself
    tgt_local = own_tgt % TB_DEV
    tgt_slot = (tgt_rel + HALF) * CAP_T + ranked(tgt_rel, tgt_local, TB_DEV)
    outbox = jax.ops.segment_sum(partial_value, tgt_slot, num_segments=span * CAP_T)
    inboxes = []
    destinations = []
    for step in range(-HALF, HALF + 1):
        bucket = outbox[(step + HALF) * CAP_T : (step + HALF + 1) * CAP_T]
        sender = myself - step
        if step == 0:
            arrived = bucket
        else:
            arrived = passed_along(bucket, ("gx", "gy"), step)
        rows = rows_of(target_ids, sender, devices, held)
        chosen, filled = picked_for(rows, TB_DEV, CAP_T, myself)
        valid = (sender >= 0) & (sender < devices)
        inboxes.append(arrived)
        destinations.append(jnp.where(filled & valid, chosen, TB_DEV))
    summed = jax.ops.segment_sum(
        jnp.concatenate(inboxes, axis=0),
        jnp.concatenate(destinations, axis=0),
        num_segments=TB_DEV + 1,
    )
    return summed[:TB_DEV].astype(jnp.bfloat16)


def solution(mesh):
    return jax.shard_map(
        body,
        mesh=mesh,
        in_specs=(P(("gx", "gy"), None, None), P(("gx", "gy"), None, None), P(), P()),
        out_specs=P(("gx", "gy"), None, None),
        check_vma=False,
    )
```

profile of v0, /device:TPU:28, one launch (start us, length us, event | category | flops | bytes accessed | tf_op | source)
XLA Modules:
  0.0 705.1 jit_solution(575367431060708103)
XLA Ops:
  0.0 0.8 compare_select_fusion.2
  0.8 22.1 %scatter_fusion.1 = s32[5,128]{1,0:T(8,128)S(1)} fusion(s32[5,128]{1,0:T(8,128)S(1)} %broadcast_in_dim.163, s32[512]{0:T(512)S(1)} %bitcast.38, s32[512]{0:T(512)S(1)} %ne.127), kind=kCustom, calls=%fused_computation.17 | custom fusion | bytes 10240 | tf_op jit(solution)/shard_map/scatter | solution.py:48
  22.9 0.3 reduce_window_sum.51
  23.2 2.5 gather_fusion.5
  25.7 0.9 fusion.39
  26.6 0.9 compare_select_fusion
  27.6 4.1 scatter_custom_fusion.6
  31.8 0.2 reduce-window.68
  32.3 3.1 gather_fusion.1
  35.5 1.5 broadcast_select_fusion.3
  37.0 1.9 collective-permute-start
  38.9 4.1 scatter_custom_fusion.7
  43.1 0.2 reduce-window.69
  43.7 3.1 gather_fusion.2
  46.8 1.5 broadcast_select_fusion.2
  48.3 3.9 collective-permute-start.1
  52.2 4.1 scatter_custom_fusion.8
  56.4 0.2 reduce-window.70
  57.0 3.1 gather_fusion.3
  60.1 1.5 broadcast_select_fusion.1
  61.7 2.0 collective-permute-start.2
  63.6 4.1 scatter_custom_fusion.9
  67.8 0.2 reduce-window.71
  68.4 3.1 gather_fusion.4
  71.5 1.6 broadcast_select_fusion
  73.1 4.8 collective-permute-start.3
  77.9 4.3 scatter_custom_fusion.2
  82.6 22.1 %scatter_fusion = s32[5,64]{1,0:T(8,128)S(1)} fusion(s32[5,64]{1,0:T(8,128)S(1)} %broadcast_in_dim.150, s32[512]{0:T(512)S(1)} %bitcast.37, s32[512]{0:T(512)S(1)} %ne.127), kind=kCustom, calls=%fused_computation.12 | custom fusion | bytes 10240 | tf_op jit(solution)/shard_map/scatter | solution.py:48
  104.6 0.2 reduce_window_sum.50
  105.1 4.1 scatter_custom_fusion.4
  109.4 4.1 scatter_custom_fusion.3
  113.7 2.6 gather_fusion
  116.3 4.1 scatter_custom_fusion.1
  120.9 12.7 %collective-permute-done = bf16[64,128,128]{2,1,0:T(8,128)(2,1)} collective-permute-done((bf16[64,128,128]{2,1,0:T(8,128)(2,1)}, bf16[64,128,128]{2,1,0:T(8,128)(2,1)}, u32[]{:S(2)}, u32[]{:S(2)}) %collective-permute-start) | collective-permute-done | bytes 2097184 | tf_op jit(solution)/shard_map/ppermute | solution.py:15
  133.6 3.2 constant_dynamic-update-slice_fusion.4
  136.8 51.7 %collective-permute-done.1 = bf16[64,128,128]{2,1,0:T(8,128)(2,1)} collective-permute-done((bf16[64,128,128]{2,1,0:T(8,128)(2,1)}, bf16[64,128,128]{2,1,0:T(8,128)(2,1)}, u32[]{:S(2)}, u32[]{:S(2)}) %collective-permute-start.1) | collective-permute-done | bytes 2097184 | tf_op jit(solution)/shard_map/ppermute | solution.py:15
  188.4 3.1 constant_dynamic-update-slice_fusion.3
  191.6 2.3 constant_dynamic-update-slice_fusion.2
  193.8 3.2 constant_dynamic-update-slice_fusion.1
  197.1 114.8 %collective-permute-done.3 = bf16[64,128,128]{2,1,0:T(8,128)(2,1)S(1)} collective-permute-done((bf16[64,128,128]{2,1,0:T(8,128)(2,1)}, bf16[64,128,128]{2,1,0:T(8,128)(2,1)S(1)}, u32[]{:S(2)}, u32[]{:S(2)}) %collective-permute-start.3) | collective-permute-done | bytes 2097184 | tf_op jit(solution)/shard_map/ppermute | solution.py:15
  311.9 1.5 constant_dynamic-update-slice_fusion
  313.4 18.5 %gather_fusion.6 = bf16[512,128,128]{2,1,0:T(8,128)(2,1)} fusion(bf16[384,128,128]{2,1,0:T(8,128)(2,1)} %constant_dynamic-update-slice_fusion, s32[1024]{0:T(1024)S(1)} %pad_clamp_fusion), kind=kCustom, calls=%fused_computation.6 | custom fusion | bytes 33556480 | tf_op jit(solution)/shard_map/gather | solution.py:83
  331.9 25.1 %convolution_bitcast_fusion = f32[512,128,128]{1,2,0:T(8,128)} fusion(bf16[512,128,128]{2,1,0:T(8,128)(2,1)} %gather_fusion.6, bf16[512,128,128]{2,1,0:T(8,128)(2,1)} %param.6), kind=kOutput, calls=%fused_computation.20 | convolution fusion | flops 2147483648 | bytes 67108864 | tf_op jit(solution)/shard_map/kts,ksc->ktc/dot_general | solution.py:84
  357.1 33.4 %copy.38 = f32[512,128,128]{2,1,0:T(8,128)} copy(f32[512,128,128]{1,2,0:T(8,128)} %convolution_bitcast_fusion) | data formatting | bytes 67108864 | tf_op jit(solution)/shard_map/kts,ksc->ktc/dot_general | solution.py:84
  390.5 3.0 broadcast_in_dim.149
  393.6 102.2 %scatter_fusion.2 = f32[80,128,128]{2,1,0:T(8,128)} fusion(f32[80,128,128]{2,1,0:T(8,128)} %broadcast_in_dim.149, s32[512]{0:T(512)S(1)} %multiply_add_fusion, f32[512,128,128]{2,1,0:T(8,128)} %copy.38), kind=kCustom, calls=%fused_computation.18 | custom fusion | flops 8388608 | bytes 100665344 | tf_op jit(solution)/shard_map/scatter-add | solution.py:91
  495.7 2.7 fusion.70
  498.4 1.9 collective-permute-start.4
  500.3 0.1 fusion.17
  500.5 3.5 collective-permute-start.5
  504.2 4.1 scatter_custom_fusion
  509.0 61.4 %collective-permute-done.4 = f32[16,128,128]{2,1,0:T(8,128)S(1)} collective-permute-done((f32[16,128,128]{2,1,0:T(8,128)}, f32[16,128,128]{2,1,0:T(8,128)S(1)}, u32[]{:S(2)}, u32[]{:S(2)}) %collective-permute-start.4) | collective-permute-done | bytes 1048608 | tf_op jit(solution)/shard_map/ppermute | solution.py:15
  570.4 1.1 constant_dynamic-update-slice_fusion.8
  571.5 1.1 constant_dynamic-update-slice_fusion.7
  572.6 3.5 fusion.69
  576.1 1.9 collective-permute-start.6
  578.1 35.9 %collective-permute-start.7 = (f32[16,128,128]{2,1,0:T(8,128)S(1)}, f32[16,128,128]{2,1,0:T(8,128)S(1)}, u32[]{:S(2)}, u32[]{:S(2)}) collective-permute-start(f32[16,128,128]{2,1,0:T(8,128)S(1)} %get-tuple-element.7), channel_id=1, source_target_pairs={{0,2},{1,3},{2,4},{3,5},{4,6},{5,7},{6,8},{7,9},{8,10},{9,11},{10,... | collective-permute-start | bytes 3145736 | tf_op jit(solution)/shard_map/ppermute | solution.py:15
  614.3 19.5 %collective-permute-done.6 = f32[16,128,128]{2,1,0:T(8,128)S(1)} collective-permute-done((f32[16,128,128]{2,1,0:T(8,128)}, f32[16,128,128]{2,1,0:T(8,128)S(1)}, u32[]{:S(2)}, u32[]{:S(2)}) %collective-permute-start.6) | collective-permute-done | bytes 1048608 | tf_op jit(solution)/shard_map/ppermute | solution.py:15
  633.9 1.1 constant_dynamic-update-slice_fusion.6
  634.9 45.9 %collective-permute-done.7 = f32[16,128,128]{2,1,0:T(8,128)S(1)} collective-permute-done((f32[16,128,128]{2,1,0:T(8,128)S(1)}, f32[16,128,128]{2,1,0:T(8,128)S(1)}, u32[]{:S(2)}, u32[]{:S(2)}) %collective-permute-start.7) | collective-permute-done | bytes 1048608 | tf_op jit(solution)/shard_map/ppermute | solution.py:15
  680.9 1.0 constant_dynamic-update-slice_fusion.5
  681.9 2.5 broadcast_in_dim.141
  684.5 16.7 %scatter_fusion.3 = f32[65,128,128]{2,1,0:T(8,128)} fusion(f32[65,128,128]{2,1,0:T(8,128)} %broadcast_in_dim.141, s32[80]{0:T(128)S(1)} %concatenate.49, f32[80,128,128]{2,1,0:T(8,128)} %constant_dynamic-update-slice_fusion.5), kind=kCustom, calls=%fused_computation.19 | custom fusion | flops 1310720 | bytes 15728960 | tf_op jit(solution)/shard_map/scatter-add | solution.py:106
  701.2 3.9 slice.79
  (77 shorter events, 4.6 us)
Async XLA Ops:
  37.0 96.6 %collective-permute-start = (bf16[64,128,128]{2,1,0:T(8,128)(2,1)}, bf16[64,128,128]{2,1,0:T(8,128)(2,1)}, u32[]{:S(2)}, u32[]{:S(2)}) collective-permute-start(bf16[64,128,128]{2,1,0:T(8,128)(2,1)} %broadcast_select_fusion.3), channel_id=1, source_target_pairs={{0,2},{1,3},{2,4},{3,5},{4,6},{5,7},{6,8},{7,9},{8,10},{9,11},{10,... | collective-permute-start | bytes 6291464 | tf_op jit(solution)/shard_map/ppermute | solution.py:15
  48.3 140.1 %collective-permute-start.1 = (bf16[64,128,128]{2,1,0:T(8,128)(2,1)}, bf16[64,128,128]{2,1,0:T(8,128)(2,1)}, u32[]{:S(2)}, u32[]{:S(2)}) collective-permute-start(bf16[64,128,128]{2,1,0:T(8,128)(2,1)} %broadcast_select_fusion.2), channel_id=1, source_target_pairs={{0,1},{1,2},{2,3},{3,4},{4,5},{5,6},{6,7},{7,8},{8,9},{9,10},{10,1... | collective-permute-start | bytes 6291464 | tf_op jit(solution)/shard_map/ppermute | solution.py:15
  61.7 132.2 %collective-permute-start.2 = (bf16[64,128,128]{2,1,0:T(8,128)(2,1)}, bf16[64,128,128]{2,1,0:T(8,128)(2,1)}, u32[]{:S(2)}, u32[]{:S(2)}) collective-permute-start(bf16[64,128,128]{2,1,0:T(8,128)(2,1)} %broadcast_select_fusion.1), channel_id=1, source_target_pairs={{1,0},{2,1},{3,2},{4,3},{5,4},{6,5},{7,6},{8,7},{9,8},{10,9},{11,1... | collective-permute-start | bytes 6291464 | tf_op jit(solution)/shard_map/ppermute | solution.py:15
  73.1 238.8 %collective-permute-start.3 = (bf16[64,128,128]{2,1,0:T(8,128)(2,1)}, bf16[64,128,128]{2,1,0:T(8,128)(2,1)S(1)}, u32[]{:S(2)}, u32[]{:S(2)}) collective-permute-start(bf16[64,128,128]{2,1,0:T(8,128)(2,1)} %broadcast_select_fusion), channel_id=1, source_target_pairs={{2,0},{3,1},{4,2},{5,3},{6,4},{7,5},{8,6},{9,7},{10,8},{11,9},{12,... | collective-permute-start | bytes 6291464 | tf_op jit(solution)/shard_map/ppermute | solution.py:15
  120.4 71.2 %copy-start = (bf16[128,128,128]{2,1,0:T(8,128)(2,1)S(1)}, bf16[128,128,128]{2,1,0:T(8,128)(2,1)}, u32[]{:S(2)}) copy-start(bf16[128,128,128]{2,1,0:T(8,128)(2,1)} %param.5) | copy-start | bytes 12582916
  498.4 72.0 %collective-permute-start.4 = (f32[16,128,128]{2,1,0:T(8,128)}, f32[16,128,128]{2,1,0:T(8,128)S(1)}, u32[]{:S(2)}, u32[]{:S(2)}) collective-permute-start(f32[16,128,128]{2,1,0:T(8,128)} %get-tuple-element.11), channel_id=1, source_target_pairs={{2,0},{3,1},{4,2},{5,3},{6,4},{7,5},{8,6},{9,7},{10,8},{11,9},{12,... | collective-permute-start | bytes 3145736 | tf_op jit(solution)/shard_map/ppermute | solution.py:15
  500.5 71.0 %collective-permute-start.5 = (f32[16,128,128]{2,1,0:T(8,128)S(1)}, f32[16,128,128]{2,1,0:T(8,128)S(1)}, u32[]{:S(2)}, u32[]{:S(2)}) collective-permute-start(f32[16,128,128]{2,1,0:T(8,128)S(1)} %get-tuple-element.10), channel_id=1, source_target_pairs={{1,0},{2,1},{3,2},{4,3},{5,4},{6,5},{7,6},{8,7},{9,8},{10,9},{11,1... | collective-permute-start | bytes 3145736 | tf_op jit(solution)/shard_map/ppermute | solution.py:15
  576.1 57.8 %collective-permute-start.6 = (f32[16,128,128]{2,1,0:T(8,128)}, f32[16,128,128]{2,1,0:T(8,128)S(1)}, u32[]{:S(2)}, u32[]{:S(2)}) collective-permute-start(f32[16,128,128]{2,1,0:T(8,128)} %get-tuple-element.8), channel_id=1, source_target_pairs={{0,1},{1,2},{2,3},{3,4},{4,5},{5,6},{6,7},{7,8},{8,9},{9,10},{10,1... | collective-permute-start | bytes 3145736 | tf_op jit(solution)/shard_map/ppermute | solution.py:15
  578.1 102.7 %collective-permute-start.7 = (f32[16,128,128]{2,1,0:T(8,128)S(1)}, f32[16,128,128]{2,1,0:T(8,128)S(1)}, u32[]{:S(2)}, u32[]{:S(2)}) collective-permute-start(f32[16,128,128]{2,1,0:T(8,128)S(1)} %get-tuple-element.7), channel_id=1, source_target_pairs={{0,2},{1,3},{2,4},{3,5},{4,6},{5,7},{6,8},{7,9},{8,10},{9,11},{10,... | collective-permute-start | bytes 3145736 | tf_op jit(solution)/shard_map/ppermute | solution.py:15
where the time goes:
time: 707 us; the launch traced here: 705 us
  waiting for transfers between devices  306 us (43%)
  other arithmetic  169 us (24%)
  local copies, waits for them, and re-layouts  148 us (21%)
  starting transfers between devices  55.7 us (8%)
  matrix products  25.1 us (4%)
    ppermute x8, waiting for transfers between devices, passed_along(): lax.ppermute(value, axis, [(source, source + steps) for source in range(i...  306 us
    scatter-add x1, other arithmetic, body(): jax.ops.segment_sum(partial_value, tgt_slot, num_segments=span * CAP_T)  102 us
    ppermute x8, starting transfers between devices, passed_along(): lax.ppermute(value, axis, [(source, source + steps) for source in range(i...  55.7 us
    scatter x2, local copies, waits for them, and re-layouts, ranked(): jnp.zeros((span, per_device), jnp.int32).at[relative + HALF, local].set(1)  44.2 us
    another operation x9, other arithmetic, picked_for(): asked = jnp.zeros((1, per_device), jnp.int32).at[0, local].max((owner ==...  36.9 us
    dot_general x1, local copies, waits for them, and re-layouts, body(): jnp.einsum('kts,ksc->ktc', weight_blocks, gathered, preferred_element_typ...  33.4 us
    dot_general x1, matrix products, body(): jnp.einsum('kts,ksc->ktc', weight_blocks, gathered, preferred_element_typ...  25.1 us
    gather x1, local copies, waits for them, and re-layouts, body(): gathered = table[index]  18.5 us
  transfers between devices with their start and end apart: 8, of which 6 were waited for; matrix products, arithmetic and copies ran while one was open for 13% of the time, Pallas kernels for 0%

commit v1 on v0

v1 whole, which is shorter than its diff:
```python
import functools

import jax
import jax.numpy as jnp
from jax import lax
from jax.experimental import pallas as pl
from jax.experimental.pallas import tpu as pltpu
from jax.sharding import PartitionSpec as P

HALF = 2
TB_DEV = 64
CAP_S = 64
CAP_T = 16
SPAN = 2 * HALF + 1
AXES = ("gx", "gy")
ARRIVALS = (-2, 2, -1, 1)
STAGES = (0,) + ARRIVALS
DEPTH = 32
UNROLL = 4
LOW_EXPONENT = -110.0


def passed_along(value, steps):
    count = lax.axis_size(AXES)
    initial, last = (max(0, -steps), min(count, count - steps))
    return lax.ppermute(value, AXES, [(source, source + steps) for source in range(initial, last)])


def rows_of(ids, device, devices, held):
    clamped = jnp.clip(device, 0, devices - 1)
    return lax.dynamic_slice_in_dim(ids, clamped * held, held, 0)


def named(rows, low, count):
    return jnp.any(rows[:, None] == low + jnp.arange(count, dtype=jnp.int32)[None, :], axis=0)


def ranks_of(asked):
    count = asked.shape[1]
    before = jnp.arange(count)[:, None] < jnp.arange(count)[None, :]
    return jnp.sum((asked[:, :, None] & before[None]).astype(jnp.int32), axis=1)


def stage_kernel(stage, last, *refs):
    bounds, packed, w_hbm, src = refs[:4]
    refs = refs[4:]
    if stage > 0:
        acc_in, refs = refs[0], refs[1:]
    if last:
        outs, acc, wbuf, sems = refs[:SPAN], refs[SPAN], refs[SPAN + 1], refs[SPAN + 2]
    else:
        acc, wbuf, sems = refs
    first = bounds[stage]
    total = bounds[stage + 1] - first

    def copy_of(i):
        slot = lax.rem(i, DEPTH)
        k = packed[first + i] // (256 * 128)
        return pltpu.make_async_copy(w_hbm.at[k], wbuf.at[slot], sems.at[slot])

    def issue(i, carry):
        copy_of(i).start()
        return carry

    lax.fori_loop(0, jnp.minimum(total, DEPTH), issue, 0)
    if stage > 0:
        acc[...] = acc_in[...]
    else:
        acc[...] = jnp.zeros_like(acc)

    def run(begin, width):
        sums = []
        for u in range(width):
            i = begin + u
            copy_of(i).wait()
            s = (packed[first + i] // 128) % 256
            sums.append(
                jnp.dot(wbuf[lax.rem(i, DEPTH)], src[s], preferred_element_type=jnp.float32)
            )
        for u in range(width):
            t = packed[first + begin + u] % 128
            acc[t] += sums[u]
        for u in range(width):
            i = begin + u + DEPTH

            @pl.when(i < total)
            def _():
                copy_of(i).start()

    def wide(g, carry):
        run(g * UNROLL, UNROLL)
        return carry

    def narrow(i, carry):
        run(i, 1)
        return carry

    groups = total // UNROLL
    lax.fori_loop(0, groups, wide, 0)
    lax.fori_loop(groups * UNROLL, total, narrow, 0)

    if last:
        for r in range(SPAN):
            if r == HALF:
                outs[r][...] = acc[r * CAP_T : (r + 1) * CAP_T]
                continue
            rows = lax.broadcasted_iota(jnp.int32, acc.shape[1:], 0)

            def encode(b, exponents, r=r):
                value = acc[r * CAP_T + b]
                most = jnp.max(jnp.abs(value), axis=0, keepdims=True)
                exponent = jnp.ceil(jnp.log(jnp.maximum(most, 1e-37)) * 1.4426950408889634)
                exponent = jnp.maximum(exponent, LOW_EXPONENT)
                scaled = jnp.floor(value * jnp.exp2(15.0 - exponent) + 0.5)
                scaled = jnp.clip(scaled, -32767.0, 32767.0)
                outs[r][b] = scaled.astype(jnp.int32).astype(jnp.int16)
                return jnp.where(rows == b, exponent.astype(jnp.int32), exponents)

            exponents = lax.fori_loop(0, CAP_T, encode, jnp.zeros(acc.shape[1:], jnp.int32))
            outs[r][CAP_T] = exponents.astype(jnp.int16)


def stage_call(stage, bounds, packed, weights, src, acc):
    last = stage == SPAN - 1
    tile = weights.shape[1:2] + src.shape[2:]
    acc_shape = (SPAN * CAP_T,) + tile
    smem = pl.BlockSpec(memory_space=pltpu.SMEM)
    vmem = pl.BlockSpec(memory_space=pltpu.VMEM)
    args = [bounds, packed, weights, src] + ([acc] if stage > 0 else [])
    in_specs = [smem, smem, pl.BlockSpec(memory_space=pl.ANY), vmem] + ([vmem] if stage > 0 else [])
    buffers = [
        pltpu.VMEM((DEPTH,) + weights.shape[1:], weights.dtype),
        pltpu.SemaphoreType.DMA((DEPTH,)),
    ]
    if last:
        out_shape = [
            jax.ShapeDtypeStruct((CAP_T,) + tile, jnp.float32)
            if r == HALF
            else jax.ShapeDtypeStruct((CAP_T + 1,) + tile, jnp.int16)
            for r in range(SPAN)
        ]
        out_specs = [vmem] * SPAN
        buffers = [pltpu.VMEM(acc_shape, jnp.float32)] + buffers
    else:
        out_shape = jax.ShapeDtypeStruct(acc_shape, jnp.float32)
        out_specs = vmem
    share = weights.shape[0] // SPAN
    return pl.pallas_call(
        functools.partial(stage_kernel, stage, last),
        out_shape=out_shape,
        in_specs=in_specs,
        out_specs=out_specs,
        scratch_shapes=buffers,
        name=f"stage_{stage}",
        cost_estimate=pl.CostEstimate(
            flops=share * 2 * 128**3, bytes_accessed=24 * 2**20, transcendentals=0
        ),
        compiler_params=pltpu.CompilerParams(vmem_limit_bytes=40 * 2**20),
    )(*args)


def final_kernel(places, *refs):
    boxes, out = refs[:SPAN], refs[SPAN]
    scales = refs[SPAN + 1]
    for s in range(SPAN):
        if s != HALF:
            scales[s] = jnp.exp2(boxes[s][CAP_T].astype(jnp.float32) - 15.0)[:CAP_T]

    def one(b, carry):
        total = jnp.zeros(out.shape[1:], jnp.float32)
        for s in range(SPAN):
            place = places[s * TB_DEV + b]
            slot = jnp.maximum(place, 0)
            if s == HALF:
                value = boxes[s][slot]
            else:
                value = boxes[s][slot].astype(jnp.float32) * scales[s, pl.ds(slot, 1), :]
            total = total + jnp.where(place >= 0, value, 0.0)
        out[b] = total.astype(out.dtype)
        return carry

    lax.fori_loop(0, TB_DEV, one, 0)


def final_call(places, boxes):
    tile = boxes[HALF].shape[1:]
    vmem = pl.BlockSpec(memory_space=pltpu.VMEM)
    return pl.pallas_call(
        final_kernel,
        out_shape=jax.ShapeDtypeStruct((TB_DEV,) + tile, jnp.bfloat16),
        in_specs=[pl.BlockSpec(memory_space=pltpu.SMEM)] + [vmem] * SPAN,
        out_specs=vmem,
        scratch_shapes=[pltpu.VMEM((SPAN, CAP_T, tile[1]), jnp.float32)],
        name="final_sum",
        compiler_params=pltpu.CompilerParams(vmem_limit_bytes=32 * 2**20),
    )(places, *boxes)


def body(source_field, weight_blocks, source_ids, target_ids):
    devices = lax.axis_size(AXES)
    myself = lax.axis_index(AXES)
    held = weight_blocks.shape[0]
    src_count = source_field.shape[0]

    asked = jnp.stack(
        [
            named(rows_of(source_ids, myself - rel, devices, held), myself * src_count, src_count)
            for rel in ARRIVALS
        ]
    )
    ranks = ranks_of(asked)
    matches = asked[:, None, :] & (
        ranks[:, None, :] == jnp.arange(CAP_S, dtype=jnp.int32)[None, :, None]
    )
    chosen = jnp.sum(
        jnp.where(matches, jnp.arange(src_count, dtype=jnp.int32)[None, None, :], 0), axis=2
    )
    arrived = []
    for n, rel in enumerate(ARRIVALS):
        arrived.append(passed_along(source_field[chosen[n]], -rel))

    own_src = rows_of(source_ids, myself, devices, held)
    low = (myself - HALF) * src_count
    own_asked = named(own_src, low, SPAN * src_count).reshape(SPAN, src_count)
    own_ranks = ranks_of(own_asked)
    is_local = (jnp.arange(SPAN) == HALF)[:, None]
    own_place = jnp.where(is_local, jnp.arange(src_count, dtype=jnp.int32)[None, :], own_ranks)
    stage_of = jnp.array([STAGES.index(r - HALF) for r in range(SPAN)], jnp.int32)
    own_place = (own_place + 256 * stage_of[:, None]).reshape(-1)
    hits = (own_src - low)[:, None] == jnp.arange(SPAN * src_count, dtype=jnp.int32)[None, :]
    staged = jnp.sum(jnp.where(hits, own_place[None, :], 0), axis=1)
    stage, place = staged // 256, staged % 256

    own_tgt = rows_of(target_ids, myself, devices, held)
    low = (myself - HALF) * TB_DEV
    tgt_asked = named(own_tgt, low, SPAN * TB_DEV).reshape(SPAN, TB_DEV)
    tgt_place = ranks_of(tgt_asked) + CAP_T * jnp.arange(SPAN, dtype=jnp.int32)[:, None]
    hits = (own_tgt - low)[:, None] == jnp.arange(SPAN * TB_DEV, dtype=jnp.int32)[None, :]
    slot = jnp.sum(jnp.where(hits, tgt_place.reshape(-1)[None, :], 0), axis=1)

    index = jnp.arange(held, dtype=jnp.int32)
    key = stage * held + index
    position = jnp.sum((key[:, None] < key[None, :]).astype(jnp.int32), axis=0)
    item = (index * 256 + place) * 128 + slot
    packed = jnp.sum(jnp.where(position[None, :] == index[:, None], item[None, :], 0), axis=1)
    bounds = jnp.sum((stage[None, :] < jnp.arange(8)[:, None]).astype(jnp.int32), axis=1)

    box_asked = []
    for step in range(-HALF, HALF + 1):
        sender = myself - step
        valid = (sender >= 0) & (sender < devices)
        rows = rows_of(target_ids, sender, devices, held)
        box_asked.append(named(rows, myself * TB_DEV, TB_DEV) & valid)
    box_asked = jnp.stack(box_asked)
    places = jnp.where(box_asked, ranks_of(box_asked), -1).reshape(-1)

    acc = None
    for n in range(SPAN):
        src = source_field if n == 0 else arrived[n - 1]
        acc = stage_call(n, bounds, packed, weight_blocks, src, acc)
    boxes = [
        acc[step + HALF] if step == 0 else passed_along(acc[step + HALF], step)
        for step in range(-HALF, HALF + 1)
    ]
    return final_call(places, boxes)


def solution(mesh):
    return jax.shard_map(
        body,
        mesh=mesh,
        in_specs=(P(AXES, None, None), P(AXES, None, None), P(), P()),
        out_specs=P(AXES, None, None),
        check_vma=False,
    )
```

time: 707 us -> 400 us (0.57)
  other arithmetic: 169 us -> 3.91 us
  local copies, waits for them, and re-layouts: 148 us -> 19.9 us
  Pallas kernels: 0 us -> 101 us
  waiting for transfers between devices: 306 us -> 218 us
  matrix products: 25.1 us -> 0 us
    scatter-add x2 -> x0, other arithmetic: 119 us -> none  [the longest x1 102 us: body(): jax.ops.segment_sum(partial_value, tgt_slot, num_segments=span * CAP_T)]
    pallas_call x0 -> x6, Pallas kernels: none -> 101 us  [the longest x5 95.1 us: stage_call(): pl.pallas_call(functools.partial(stage_kernel, stage, last), out_shape=ou...]
    ppermute x8, waiting for transfers between devices: 306 us -> 218 us  [passed_along(): lax.ppermute(value, AXES, [(source, source + steps) for source in range(i...]
    scatter x2 -> x0, local copies, waits for them, and re-layouts: 44.2 us -> none  [ranked(): jnp.zeros((span, per_device), jnp.int32).at[relative + HALF, local].set(1)]
    another operation x20 -> x1, other arithmetic: 38.6 us -> 0.01 us  [body(): jnp.stack([named(rows_of(source_ids, myself - rel, devices, held), myself...]
    dot_general x1 -> x0, local copies, waits for them, and re-layouts: 33.4 us -> none  [body(): jnp.einsum('kts,ksc->ktc', weight_blocks, gathered, preferred_element_typ...]
    dot_general x1 -> x0, matrix products: 25.1 us -> none  [body(): jnp.einsum('kts,ksc->ktc', weight_blocks, gathered, preferred_element_typ...]
    gather x7 -> x4, local copies, waits for them, and re-layouts: 36.2 us -> 17.4 us  [body(): arrived.append(passed_along(source_field[chosen[n]], -rel))]
  transfers between devices with their start and end apart: 8 -> 8, of which waited for: 6 -> 4; matrix products, arithmetic and copies ran while one was open for 13% -> 4% of each run, Pallas kernels for 0% -> 19%
where the time goes in v1:
time: 400 us; the launch traced here: 393 us
  waiting for transfers between devices  218 us (54%)
  Pallas kernels  101 us (25%)
  starting transfers between devices  49.8 us (12%)
  local copies, waits for them, and re-layouts  19.9 us (5%)
    ppermute x8, waiting for transfers between devices, passed_along(): lax.ppermute(value, AXES, [(source, source + steps) for source in range(i...  218 us
    pallas_call x5, Pallas kernels, stage_call(): pl.pallas_call(functools.partial(stage_kernel, stage, last), out_shape=ou...  95.1 us
    ppermute x8, starting transfers between devices, passed_along(): lax.ppermute(value, AXES, [(source, source + steps) for source in range(i...  49.8 us
    gather x4, local copies, waits for them, and re-layouts, body(): arrived.append(passed_along(source_field[chosen[n]], -rel))  17.4 us
  transfers between devices with their start and end apart: 8, of which 4 were waited for; matrix products, arithmetic and copies ran while one was open for 4% of the time, Pallas kernels for 19%

profile of v1, /device:TPU:28, one launch (start us, length us, event | category | flops | bytes accessed | tf_op | source)
XLA Modules:
  0.0 392.6 jit_solution(922873634284878452)
XLA Ops:
  0.0 0.9 broadcast_subtract_fusion
  1.0 0.4 compare_reduce_fusion.5
  1.3 0.1 convert_reduce_fusion.2
  1.5 0.2 select_reduce_fusion.3
  1.7 4.4 %gather_fusion.3 = bf16[64,128,128]{2,1,0:T(8,128)(2,1)} fusion(bf16[128,128,128]{2,1,0:T(8,128)(2,1)} %refs_3_.1, s32[1024]{0:T(1024)S(1)} %pad_clamp_fusion), kind=kCustom, calls=%fused_computation.3 | custom fusion | bytes 4194560 | tf_op jit(solution)/shard_map/gather | solution.py:220
  6.1 1.9 collective-permute-start.3
  8.0 4.3 %gather_fusion.2 = bf16[64,128,128]{2,1,0:T(8,128)(2,1)} fusion(bf16[128,128,128]{2,1,0:T(8,128)(2,1)} %refs_3_.1, s32[1024]{0:T(1024)S(1)} %pad_clamp_fusion.1), kind=kCustom, calls=%fused_computation.2 | custom fusion | bytes 4194560 | tf_op jit(solution)/shard_map/gather | solution.py:220
  12.3 4.8 %collective-permute-start.2 = (bf16[64,128,128]{2,1,0:T(8,128)(2,1)}, bf16[64,128,128]{2,1,0:T(8,128)(2,1)}, u32[]{:S(2)}, u32[]{:S(2)}) collective-permute-start(bf16[64,128,128]{2,1,0:T(8,128)(2,1)} %gather_fusion.2), channel_id=1, source_target_pairs={{2,0},{3,1},{4,2},{5,3},{6,4},{7,5},{8,6},{9,7},{10,8},{11,9},{12,... | collective-permute-start | bytes 6291464 | tf_op jit(solution)/shard_map/ppermute | solution.py:26
  17.2 4.4 %gather_fusion.1 = bf16[64,128,128]{2,1,0:T(8,128)(2,1)} fusion(bf16[128,128,128]{2,1,0:T(8,128)(2,1)} %refs_3_.1, s32[1024]{0:T(1024)S(1)} %pad_clamp_fusion.2), kind=kCustom, calls=%fused_computation.1 | custom fusion | bytes 4194560 | tf_op jit(solution)/shard_map/gather | solution.py:220
  21.5 1.9 collective-permute-start.1
  23.4 0.0 copy-start.1
  23.5 4.3 %gather_fusion = bf16[64,128,128]{2,1,0:T(8,128)(2,1)} fusion(bf16[128,128,128]{2,1,0:T(8,128)(2,1)} %refs_3_.1, s32[1024]{0:T(1024)S(1)} %pad_clamp_fusion.3), kind=kCustom, calls=%fused_computation | custom fusion | bytes 4194560 | tf_op jit(solution)/shard_map/gather | solution.py:220
  27.8 3.9 collective-permute-start
  31.8 0.2 compare_reduce_fusion.1
  32.0 0.3 compare_reduce_fusion.6
  32.4 0.1 and.229
  32.5 0.2 convert_reduce_fusion.3
  32.6 0.1 broadcast_add_fusion
  32.7 0.1 add.223
  32.8 0.3 compare_reduce_fusion
  33.1 0.2 convert_reduce_fusion.1
  33.2 0.2 select_reduce_fusion.2
  33.4 0.0 copy-done.1
  33.4 0.1 add_bitcast_fusion
  33.5 0.3 select_reduce_fusion
  33.8 0.1 convert_reduce_fusion.5.refs_0_
  33.9 0.2 convert_reduce_fusion
  34.1 0.2 select_reduce_fusion.1.refs_1_
  34.3 0.0 copy-start
  34.3 2.2 copy-done
  36.5 24.7 %stage_0.1.refs_4_ = f32[80,128,128]{2,1,0:T(8,128)S(1)} custom-call(s32[8]{0:T(128)S(1)} %convert_reduce_fusion.5.refs_0_, s32[512]{0:T(512)S(1)} %select_reduce_fusion.1.refs_1_, bf16[512,128,128]{2,1,0:T(8,128)(2,1)} %refs_2_.9, bf16[128,128,128]{2,1,0:T(8,128)(2,1)S(1)} %copy-done), custom_call_target="tpu_custom_call" | custom-call | flops 427819008 | bytes 25165824 | tf_op jit(solution)/shard_map/stage_0/pallas_call | solution.py:148
  61.2 86.3 %collective-permute-done.3.refs_3_ = bf16[64,128,128]{2,1,0:T(8,128)(2,1)} collective-permute-done((bf16[64,128,128]{2,1,0:T(8,128)(2,1)}, bf16[64,128,128]{2,1,0:T(8,128)(2,1)}, u32[]{:S(2)}, u32[]{:S(2)}) %collective-permute-start.3) | collective-permute-done | bytes 2097184 | tf_op jit(solution)/shard_map/ppermute | solution.py:26
  147.5 17.1 %stage_1.1.refs_4_ = f32[80,128,128]{2,1,0:T(8,128)S(1)} custom-call(s32[8]{0:T(128)S(1)} %convert_reduce_fusion.5.refs_0_, s32[512]{0:T(512)S(1)} %select_reduce_fusion.1.refs_1_, bf16[512,128,128]{2,1,0:T(8,128)(2,1)} %refs_2_.9, bf16[64,128,128]{2,1,0:T(8,128)(2,1)} %collective-permute-done.3.refs_3_, f32[80,128,128]{2,1,0:T(8,128)S(1)} %stage_0.1.refs_4_), custom_call_target="tpu_custom_call" | custom-call | flops 427819008 | bytes 25165824 | tf_op jit(solution)/shard_map/stage_1/pallas_call | solution.py:148
  164.6 71.4 %collective-permute-done.2.refs_3_ = bf16[64,128,128]{2,1,0:T(8,128)(2,1)} collective-permute-done((bf16[64,128,128]{2,1,0:T(8,128)(2,1)}, bf16[64,128,128]{2,1,0:T(8,128)(2,1)}, u32[]{:S(2)}, u32[]{:S(2)}) %collective-permute-start.2) | collective-permute-done | bytes 2097184 | tf_op jit(solution)/shard_map/ppermute | solution.py:26
  236.1 17.9 %stage_2.1.refs_4_ = f32[80,128,128]{2,1,0:T(8,128)S(1)} custom-call(s32[8]{0:T(128)S(1)} %convert_reduce_fusion.5.refs_0_, s32[512]{0:T(512)S(1)} %select_reduce_fusion.1.refs_1_, bf16[512,128,128]{2,1,0:T(8,128)(2,1)} %refs_2_.9, bf16[64,128,128]{2,1,0:T(8,128)(2,1)} %collective-permute-done.2.refs_3_, f32[80,128,128]{2,1,0:T(8,128)S(1)} %stage_1.1.refs_4_), custom_call_target="tpu_custom_call" | custom-call | flops 427819008 | bytes 25165824 | tf_op jit(solution)/shard_map/stage_2/pallas_call | solution.py:148
  254.0 0.0 collective-permute-done.1.refs_3_
  254.0 15.4 %stage_3.1.refs_4_ = f32[80,128,128]{2,1,0:T(8,128)S(1)} custom-call(s32[8]{0:T(128)S(1)} %convert_reduce_fusion.5.refs_0_, s32[512]{0:T(512)S(1)} %select_reduce_fusion.1.refs_1_, bf16[512,128,128]{2,1,0:T(8,128)(2,1)} %refs_2_.9, bf16[64,128,128]{2,1,0:T(8,128)(2,1)} %collective-permute-done.1.refs_3_, f32[80,128,128]{2,1,0:T(8,128)S(1)} %stage_2.1.refs_4_), custom_call_target="tpu_custom_call" | custom-call | flops 427819008 | bytes 25165824 | tf_op jit(solution)/shard_map/stage_3/pallas_call | solution.py:148
  269.4 0.0 collective-permute-done.refs_3_
  269.4 20.1 %stage_4.1 = (s16[17,128,128]{2,1,0:T(8,128)(2,1)}, s16[17,128,128]{2,1,0:T(8,128)(2,1)}, f32[16,128,128]{2,1,0:T(8,128)S(1)}, s16[17,128,128]{2,1,0:T(8,128)(2,1)}, s16[17,128,128]{2,1,0:T(8,128)(2,1)}) custom-call(s32[8]{0:T(128)S(1)} %convert_reduce_fusion.5.refs_0_, s32[512]{0:T(512)S(1)} %select_reduce_fusion.1.refs_1_, bf16[512,128,128]{2,1,0:T(8,128)(2,1)} %refs_2_.9, ...), custom_call_target="tpu_custom_call" | custom-call | flops 427819008 | bytes 25165824 | tf_op jit(solution)/shard_map/stage_4/pallas_call | solution.py:148
  289.5 26.7 %collective-permute-start.4 = (s16[17,128,128]{2,1,0:T(8,128)(2,1)}, s16[17,128,128]{2,1,0:T(8,128)(2,1)S(1)}, u32[]{:S(2)}, u32[]{:S(2)}) collective-permute-start(s16[17,128,128]{2,1,0:T(8,128)(2,1)} %get-tuple-element.10), channel_id=1, source_target_pairs={{2,0},{3,1},{4,2},{5,3},{6,4},{7,5},{8,6},{9,7},{10,8},{11,9},{12,... | collective-permute-start | bytes 1671176 | tf_op jit(solution)/shard_map/ppermute | solution.py:26
  316.2 4.0 %collective-permute-start.5 = (s16[17,128,128]{2,1,0:T(8,128)(2,1)}, s16[17,128,128]{2,1,0:T(8,128)(2,1)S(1)}, u32[]{:S(2)}, u32[]{:S(2)}) collective-permute-start(s16[17,128,128]{2,1,0:T(8,128)(2,1)} %get-tuple-element.11), channel_id=1, source_target_pairs={{1,0},{2,1},{3,2},{4,3},{5,4},{6,5},{7,6},{8,7},{9,8},{10,9},{11,1... | collective-permute-start | bytes 1671176 | tf_op jit(solution)/shard_map/ppermute | solution.py:26
  320.3 4.0 %collective-permute-start.6 = (s16[17,128,128]{2,1,0:T(8,128)(2,1)}, s16[17,128,128]{2,1,0:T(8,128)(2,1)S(1)}, u32[]{:S(2)}, u32[]{:S(2)}) collective-permute-start(s16[17,128,128]{2,1,0:T(8,128)(2,1)} %get-tuple-element.13), channel_id=1, source_target_pairs={{0,1},{1,2},{2,3},{3,4},{4,5},{5,6},{6,7},{7,8},{8,9},{9,10},{10,1... | collective-permute-start | bytes 1671176 | tf_op jit(solution)/shard_map/ppermute | solution.py:26
  324.2 2.5 collective-permute-start.7
  326.8 0.1 select_n.127.places
  326.9 33.7 %collective-permute-done.4.refs_0_ = s16[17,128,128]{2,1,0:T(8,128)(2,1)S(1)} collective-permute-done((s16[17,128,128]{2,1,0:T(8,128)(2,1)}, s16[17,128,128]{2,1,0:T(8,128)(2,1)S(1)}, u32[]{:S(2)}, u32[]{:S(2)}) %collective-permute-start.4) | collective-permute-done | bytes 557088 | tf_op jit(solution)/shard_map/ppermute | solution.py:26
  360.6 0.0 collective-permute-done.5.refs_1_
  360.6 0.0 collective-permute-done.6.refs_3_
  360.6 26.0 %collective-permute-done.7.refs_4_ = s16[17,128,128]{2,1,0:T(8,128)(2,1)} collective-permute-done((s16[17,128,128]{2,1,0:T(8,128)(2,1)}, s16[17,128,128]{2,1,0:T(8,128)(2,1)}, u32[]{:S(2)}, u32[]{:S(2)}) %collective-permute-start.7) | collective-permute-done | bytes 557088 | tf_op jit(solution)/shard_map/ppermute | solution.py:26
  386.7 5.9 %final_sum.1 = bf16[64,128,128]{2,1,0:T(8,128)(2,1)} custom-call(s32[320]{0:T(512)S(1)} %select_n.127.places, s16[17,128,128]{2,1,0:T(8,128)(2,1)S(1)} %collective-permute-done.4.refs_0_, s16[17,128,128]{2,1,0:T(8,128)(2,1)S(1)} %collective-permute-done.5.refs_1_, f32[16,128,128]{2,1,0:T(8,128)S(1)} %get-tuple-element.12.refs_2_, ...), custom_call_target="tpu_custom_call" | custom-call | tf_op jit(solution)/shard_map/final_sum/pallas_call | solution.py:188
  (22 shorter events, 0.2 us)
Async XLA Ops:
  6.1 141.5 %collective-permute-start.3 = (bf16[64,128,128]{2,1,0:T(8,128)(2,1)}, bf16[64,128,128]{2,1,0:T(8,128)(2,1)}, u32[]{:S(2)}, u32[]{:S(2)}) collective-permute-start(bf16[64,128,128]{2,1,0:T(8,128)(2,1)} %gather_fusion.3), channel_id=1, source_target_pairs={{0,2},{1,3},{2,4},{3,5},{4,6},{5,7},{6,8},{7,9},{8,10},{9,11},{10,... | collective-permute-start | bytes 6291464 | tf_op jit(solution)/shard_map/ppermute | solution.py:26
  12.3 223.8 %collective-permute-start.2 = (bf16[64,128,128]{2,1,0:T(8,128)(2,1)}, bf16[64,128,128]{2,1,0:T(8,128)(2,1)}, u32[]{:S(2)}, u32[]{:S(2)}) collective-permute-start(bf16[64,128,128]{2,1,0:T(8,128)(2,1)} %gather_fusion.2), channel_id=1, source_target_pairs={{2,0},{3,1},{4,2},{5,3},{6,4},{7,5},{8,6},{9,7},{10,8},{11,9},{12,... | collective-permute-start | bytes 6291464 | tf_op jit(solution)/shard_map/ppermute | solution.py:26
  21.5 232.4 %collective-permute-start.1 = (bf16[64,128,128]{2,1,0:T(8,128)(2,1)}, bf16[64,128,128]{2,1,0:T(8,128)(2,1)}, u32[]{:S(2)}, u32[]{:S(2)}) collective-permute-start(bf16[64,128,128]{2,1,0:T(8,128)(2,1)} %gather_fusion.1), channel_id=1, source_target_pairs={{0,1},{1,2},{2,3},{3,4},{4,5},{5,6},{6,7},{7,8},{8,9},{9,10},{10,1... | collective-permute-start | bytes 6291464 | tf_op jit(solution)/shard_map/ppermute | solution.py:26
  23.4 10.0 %copy-start.1 = (s32[5]{0:T(128)S(1)}, s32[5]{0:T(128)}, u32[]{:S(2)}) copy-start(s32[5]{0:T(128)} %constant.76) | copy-start | bytes 64
  27.8 241.6 %collective-permute-start = (bf16[64,128,128]{2,1,0:T(8,128)(2,1)}, bf16[64,128,128]{2,1,0:T(8,128)(2,1)S(1)}, u32[]{:S(2)}, u32[]{:S(2)}) collective-permute-start(bf16[64,128,128]{2,1,0:T(8,128)(2,1)} %gather_fusion), channel_id=1, source_target_pairs={{1,0},{2,1},{3,2},{4,3},{5,4},{6,5},{7,6},{8,7},{9,8},{10,9},{11,1... | collective-permute-start | bytes 6291464 | tf_op jit(solution)/shard_map/ppermute | solution.py:26
  34.3 2.2 copy-start
  289.5 71.1 %collective-permute-start.4 = (s16[17,128,128]{2,1,0:T(8,128)(2,1)}, s16[17,128,128]{2,1,0:T(8,128)(2,1)S(1)}, u32[]{:S(2)}, u32[]{:S(2)}) collective-permute-start(s16[17,128,128]{2,1,0:T(8,128)(2,1)} %get-tuple-element.10), channel_id=1, source_target_pairs={{2,0},{3,1},{4,2},{5,3},{6,4},{7,5},{8,6},{9,7},{10,8},{11,9},{12,... | collective-permute-start | bytes 1671176 | tf_op jit(solution)/shard_map/ppermute | solution.py:26
  316.2 44.4 %collective-permute-start.5 = (s16[17,128,128]{2,1,0:T(8,128)(2,1)}, s16[17,128,128]{2,1,0:T(8,128)(2,1)S(1)}, u32[]{:S(2)}, u32[]{:S(2)}) collective-permute-start(s16[17,128,128]{2,1,0:T(8,128)(2,1)} %get-tuple-element.11), channel_id=1, source_target_pairs={{1,0},{2,1},{3,2},{4,3},{5,4},{6,5},{7,6},{8,7},{9,8},{10,9},{11,1... | collective-permute-start | bytes 1671176 | tf_op jit(solution)/shard_map/ppermute | solution.py:26
  320.3 40.4 %collective-permute-start.6 = (s16[17,128,128]{2,1,0:T(8,128)(2,1)}, s16[17,128,128]{2,1,0:T(8,128)(2,1)S(1)}, u32[]{:S(2)}, u32[]{:S(2)}) collective-permute-start(s16[17,128,128]{2,1,0:T(8,128)(2,1)} %get-tuple-element.13), channel_id=1, source_target_pairs={{0,1},{1,2},{2,3},{3,4},{4,5},{5,6},{6,7},{7,8},{8,9},{9,10},{10,1... | collective-permute-start | bytes 1671176 | tf_op jit(solution)/shard_map/ppermute | solution.py:26
  324.2 62.4 %collective-permute-start.7 = (s16[17,128,128]{2,1,0:T(8,128)(2,1)}, s16[17,128,128]{2,1,0:T(8,128)(2,1)}, u32[]{:S(2)}, u32[]{:S(2)}) collective-permute-start(s16[17,128,128]{2,1,0:T(8,128)(2,1)} %get-tuple-element.14), channel_id=1, source_target_pairs={{0,2},{1,3},{2,4},{3,5},{4,6},{5,7},{6,8},{7,9},{8,10},{9,11},{10,... | collective-permute-start | bytes 1671176 | tf_op jit(solution)/shard_map/ppermute | solution.py:26
